TPU v7x, 256 devices: a whole 4x4x8 slice. The times are simulated.
256 devices in a mesh: seq: 32 (over y, z), mp: 8 (over x, core).
Axes of the slice: x: 4, y: 4, z: 8, core: 2. Of those that a mesh axis runs over, the one named last changes fastest.
Arguments:
- tokens: bfloat16 [12288, 2048], P('seq'), may hold values from -24 to 24
- database: bfloat16 [256, 96, 896], P('seq'), may hold values from -24 to 24
- nb_shard: int32 [192, 2], replicated, may hold values from 0 to 31, all different within a row; in each aligned block of 6 rows (0 to 5, 6 to 11, ...) no two rows name the same one
- nb_row: int32 [192, 2], replicated, may hold values from 0 to 7
- dec_gain: float32 [2048], replicated, may hold values from 0.1 to 1.9
- enc_gain: float32 [896], replicated, may hold values from 0.1 to 1.9
- w_in: bfloat16 [896, 1792], replicated, may hold values from -0.1875 to 0.1875
- w_out: bfloat16 [1792, 896], replicated, may hold values from -0.125 to 0.125
- w_query: bfloat16 [2048, 2048], P(None, 'mp'), may hold values from -0.125 to 0.125
- w_key: bfloat16 [896, 2048], P(None, 'mp'), may hold values from -0.1875 to 0.1875
- w_value: bfloat16 [896, 2048], P(None, 'mp'), may hold values from -0.1875 to 0.1875
- w_proj: bfloat16 [2048, 2048], P('mp'), may hold values from -0.5 to 0.5
- grad_out: bfloat16 [12288, 2048], P('seq'), may hold values from -6 to 6
Outputs:
- cca: bfloat16 [12288, 2048], P('seq', 'mp')
- grad_tokens: float32 [12288, 2048], P('seq', 'mp')
- grad_database: float32 [256, 96, 896], P('seq', 'mp')
Inputs may be any that keep to these rules, and one draw needn't show every extreme that they name: `nb_shard`: in each aligned block of 6 stretches (the stretches of one device) no shard is named more than 1 times, and some block reaches it; the 2 neighbours of a stretch come from different shards.
All inputs are finite; a program needn't handle non-finite values.
Results may differ from a plain program's by a relative error of at most 0.017.
Values may be sent and summed in bfloat16 or wider, within the bound.
A program may use at most 128 MiB of HBM per device.

v0:
```python
import jax
import jax.numpy as jnp
from jax import lax
from jax.sharding import Mesh
from jax.sharding import PartitionSpec as P

HD = 128
L = 96
STRETCH = 64
K = 2
SEQ_LEN = 4096
MP = ("mp_0", "mp_1")
EPSILON = 1e-06


def cut_rows(length, count):
    unit = 8 if length >= 8 * count else 1
    return [length // unit * k // count * unit for k in range(1, count)]


def gather_in_order(x, axes, sequence):
    tiles = x[None]
    for k in sequence:
        tiles = lax.all_gather(tiles, axes[k], axis=0, tiled=True)
    block = [lax.axis_size(axes[k]) for k in reversed(sequence)]
    tiles = tiles.reshape(*block, *x.shape)
    turned = sorted(range(len(sequence)), key=lambda place: sequence[len(sequence) - 1 - place])
    return tiles.transpose(*turned, *range(len(sequence), tiles.ndim)).reshape(-1, *x.shape)


def joined_along(tiles, dim):
    shape = list(tiles.shape[1:])
    shape[dim] *= tiles.shape[0]
    return jnp.moveaxis(tiles, 0, dim).reshape(shape)


def spread_gather(x, axes, dim):
    widest = max(range(max(1, x.ndim - 1)), key=lambda d: x.shape[d])
    count, outs = (len(axes), [])
    for leading, section in enumerate(jnp.split(x, cut_rows(x.shape[widest], count), axis=widest)):
        if section.size:
            sequence = [(leading - k) % count for k in range(count)]
            outs.append(gather_in_order(section, axes, sequence))
    return joined_along(jnp.concatenate(outs, axis=widest + 1), dim)


def split_up(x, dim, devices):
    shape = x.shape
    tiles = x.reshape(*shape[:dim], devices, shape[dim] // devices, *shape[dim + 1 :])
    return jnp.moveaxis(tiles, dim, 0)


def summed_on_arrival(x, axis, dim):
    devices = lax.axis_size(axis)
    tiles = lax.all_to_all(split_up(x, dim, devices), axis, 0, 0, tiled=True)
    return jnp.sum(tiles.astype(jnp.float32), axis=0)


def in_one_piece(arrays, axis, dim, along):
    both = jnp.concatenate(arrays, axis=along)
    out, at, outs = (lax.psum_scatter(both, axis, scatter_dimension=dim, tiled=True), 0, [])
    for a in arrays:
        outs.append(lax.slice_in_dim(out, at, at + a.shape[along], axis=along))
        at += a.shape[along]
    return tuple(outs)


def rms_scaling(values):
    return lax.rsqrt(jnp.mean(values * values, axis=-1, keepdims=True) + EPSILON)


def silu_slope(pre_act):
    sigmoid = jax.nn.sigmoid(pre_act)
    return sigmoid * (1.0 + pre_act * (1.0 - sigmoid))


def dot_t(matrix, weight):
    return lax.dot_general(
        matrix, weight, (((1,), (1,)), ((), ())), preferred_element_type=jnp.float32
    )


def encode(embedded, enc_gain, w_in, w_out):
    values = embedded.astype(jnp.float32)
    scaling = rms_scaling(values)
    normed = (values * scaling * enc_gain).astype(jnp.bfloat16)
    pre_act = jnp.einsum("nle,ef->nlf", normed, w_in, preferred_element_type=jnp.float32)
    hidden = jax.nn.silu(pre_act).astype(jnp.bfloat16)
    mixed = jnp.einsum("nlf,fe->nle", hidden, w_out, preferred_element_type=jnp.float32)
    encoded = (values + mixed).astype(jnp.bfloat16)
    return (encoded, pre_act, scaling)


def encode_back(embedded, pre_act, scaling, grad_enc, enc_gain, w_in, w_out):
    grad_hidden = jnp.einsum(
        "nle,fe->nlf", grad_enc.astype(jnp.bfloat16), w_out, preferred_element_type=jnp.float32
    )
    grad_pre = (grad_hidden * silu_slope(pre_act)).astype(jnp.bfloat16)
    grad_unit = (
        jnp.einsum("nlf,ef->nle", grad_pre, w_in, preferred_element_type=jnp.float32) * enc_gain
    )
    unit_rows = embedded.astype(jnp.float32) * scaling
    return grad_enc + scaling * (
        grad_unit - unit_rows * jnp.mean(grad_unit * unit_rows, axis=-1, keepdims=True)
    )


def body(
    tokens,
    database,
    nb_shard,
    nb_row,
    dec_gain,
    enc_gain,
    w_in,
    w_out,
    w_query,
    w_key,
    w_value,
    w_proj,
    grad_out,
):
    seq_count = lax.axis_size("seq")
    my_seq = lax.axis_index("seq")
    mp_count = lax.axis_size(MP)
    my_mp = lax.axis_index(MP)
    tok_rows = tokens.shape[0]
    stretches_here = tok_rows // STRETCH
    width = w_query.shape[1]
    heads_here = width // HD
    nb_here = stretches_here * K
    slot_cap = max(1, (nb_here + seq_count - 1) // seq_count)
    slot_count = seq_count * slot_cap
    tok_span = database.shape[1] // mp_count
    tok_start = my_mp * tok_span
    requests = nb_shard.reshape(seq_count, nb_here)
    req_rows = nb_row.reshape(seq_count, nb_here)
    req_order = jnp.arange(nb_here)
    same_shard = requests[:, :, None] == requests[:, None, :]
    before = req_order[None, :] < req_order[:, None]
    slot_rank = jnp.sum((same_shard & before[None]).astype(jnp.int32), axis=2)
    held_here = requests == my_seq
    slot_ids = jnp.arange(slot_cap)
    slot_pick = held_here[:, None, :] & (slot_rank[:, None, :] == slot_ids[None, :, None])
    slot_row = jnp.sum(slot_pick.astype(jnp.int32) * req_rows[:, None, :], axis=2).reshape(
        slot_count
    )
    slot_live = jnp.any(slot_pick, axis=2).reshape(slot_count)
    own_req = lax.dynamic_index_in_dim(requests, my_seq, 0, keepdims=False)
    own_rank = lax.dynamic_index_in_dim(slot_rank, my_seq, 0, keepdims=False)
    source = own_req * slot_cap + own_rank
    kv_weight = jnp.concatenate([w_key, w_value], axis=1)
    own_slice = lax.dynamic_slice_in_dim(database, tok_start, tok_span, 1)
    outgoing = jnp.take(own_slice, slot_row, axis=0)
    arrived = lax.all_to_all(outgoing, "seq", split_axis=0, concat_axis=0, tiled=True)
    embed_part = jnp.take(arrived, source, axis=0)
    enc_part, pre_part, scale_part = encode(embed_part, enc_gain, w_in, w_out)
    kv_rows = jnp.einsum(
        "nle,ef->nlf", spread_gather(enc_part, MP, 1), kv_weight, preferred_element_type=jnp.float32
    ).astype(jnp.bfloat16)
    key_rows = kv_rows[:, :, :width]
    value_rows = kv_rows[:, :, width:]
    tok_vals = tokens.astype(jnp.float32)
    tok_scaling = rms_scaling(tok_vals)
    tok_unit = tok_vals * tok_scaling
    tok_normed = (tok_unit * dec_gain).astype(jnp.bfloat16)
    query_rows = jnp.dot(tok_normed, w_query, preferred_element_type=jnp.float32).astype(
        jnp.bfloat16
    )
    query_blk = query_rows.reshape(stretches_here, STRETCH, heads_here, HD)
    key_blk = key_rows.reshape(stretches_here, K * L, heads_here, HD)
    value_blk = value_rows.reshape(stretches_here, K * L, heads_here, HD)
    factor = HD ** (-0.5)
    scores = (
        jnp.einsum("cqhd,ckhd->chqk", query_blk, key_blk, preferred_element_type=jnp.float32)
        * factor
    )
    exp_score = jnp.exp(scores)
    attn_prob = exp_score / jnp.sum(exp_score, axis=-1, keepdims=True)
    attn_weight = attn_prob.astype(jnp.bfloat16)
    context = (
        jnp.einsum("chqk,ckhd->cqhd", attn_weight, value_blk, preferred_element_type=jnp.float32)
        .astype(jnp.bfloat16)
        .reshape(tok_rows, width)
    )
    stretch_pos = (my_seq * stretches_here + jnp.arange(stretches_here)) % (SEQ_LEN // STRETCH)
    live_tok = jnp.repeat(stretch_pos != 0, STRETCH)[:, None]
    out_terms = jnp.where(
        live_tok, jnp.dot(context, w_proj, preferred_element_type=jnp.float32), 0.0
    )
    masked = jnp.where(live_tok, grad_out, jnp.zeros_like(grad_out))
    grad_ctx = dot_t(masked, w_proj).astype(jnp.bfloat16)
    grad_blk = grad_ctx.reshape(stretches_here, STRETCH, heads_here, HD)
    grad_prob = jnp.einsum(
        "cqhd,ckhd->chqk", grad_blk, value_blk, preferred_element_type=jnp.float32
    )
    grad_score = (
        attn_prob * (grad_prob - jnp.sum(attn_prob * grad_prob, axis=-1, keepdims=True)) * factor
    ).astype(jnp.bfloat16)
    grad_value = jnp.einsum(
        "chqk,cqhd->ckhd", attn_weight, grad_blk, preferred_element_type=jnp.float32
    ).astype(jnp.bfloat16)
    grad_query = (
        jnp.einsum("chqk,ckhd->cqhd", grad_score, key_blk, preferred_element_type=jnp.float32)
        .astype(jnp.bfloat16)
        .reshape(tok_rows, width)
    )
    grad_key = jnp.einsum(
        "chqk,cqhd->ckhd", grad_score, query_blk, preferred_element_type=jnp.float32
    ).astype(jnp.bfloat16)
    key_grad = grad_key.reshape(nb_here, L, width)
    value_grad = grad_value.reshape(nb_here, L, width)
    enc_terms = jnp.einsum("nlf,ef->nle", key_grad, w_key, preferred_element_type=jnp.float32)
    enc_terms = enc_terms + jnp.einsum(
        "nlf,ef->nle", value_grad, w_value, preferred_element_type=jnp.float32
    )
    grad_enc = summed_on_arrival(enc_terms.astype(jnp.bfloat16), MP, 1)
    grad_normed = dot_t(grad_query, w_query)
    tok_grad = grad_normed * dec_gain
    tok_terms = tok_scaling * (
        tok_grad - tok_unit * jnp.mean(tok_grad * tok_unit, axis=-1, keepdims=True)
    )
    grad_embed = encode_back(embed_part, pre_part, scale_part, grad_enc, enc_gain, w_in, w_out)
    place_back = (source[:, None] == jnp.arange(slot_count)[None, :]).astype(jnp.float32)
    returned = jnp.einsum("ns,nle->sle", place_back, grad_embed, precision=lax.Precision.HIGHEST)
    received = lax.all_to_all(
        returned.astype(jnp.bfloat16), "seq", split_axis=0, concat_axis=0, tiled=True
    ).astype(returned.dtype)
    row_hit = (
        (slot_row[None, :] == jnp.arange(database.shape[0])[:, None]) & slot_live[None, :]
    ).astype(jnp.float32)
    grad_database = jnp.einsum("rs,sle->rle", row_hit, received, precision=lax.Precision.HIGHEST)
    cca_sum, grad_sum = tuple(
        (
            part.astype(jnp.float32)
            for part in in_one_piece(
                (out_terms.astype(jnp.bfloat16), tok_terms.astype(jnp.bfloat16)), MP, 1, 0
            )
        )
    )
    return (cca_sum.astype(jnp.bfloat16), grad_sum, grad_database)


def solution(mesh):
    split = Mesh(mesh.devices.reshape(mesh.shape["seq"], 4, 2), ("seq", "mp_0", "mp_1"))
    placed = (
        P("seq", None),
        P("seq", None, None),
        P(),
        P(),
        P(),
        P(),
        P(),
        P(),
        P(None, MP),
        P(None, MP),
        P(None, MP),
        P(MP, None),
        P("seq", None),
    )
    return jax.shard_map(
        body,
        mesh=split,
        in_specs=placed,
        out_specs=(P("seq", MP), P("seq", MP), P("seq", MP, None)),
        check_vma=False,
    )
```

profile of v0, /device:TPU:32, one launch (start us, length us, event | category | flops | bytes accessed | tf_op | source)
XLA Modules:
  0.0 251.1 jit_solution(8221677842646894722)
XLA Ops:
  16.6 11.5 %all-to-all-start = ((bf16[32,12,896]{2,1,0:T(8,128)(2,1)}), bf16[32,12,896]{2,1,0:T(8,128)(2,1)}, u32[]{:S(2)}, u32[]{:S(2)}) async-start(bf16[32,12,896]{2,1,0:T(8,128)(2,1)} %broadcast_select_fusion), calls=%async_computation | async-start | bytes 1835008 | tf_op jit(solution)/shard_map/all_to_all | solution.py:155
  37.7 16.4 %all-to-all-done = bf16[32,12,896]{2,1,0:T(8,128)(2,1)} async-done(((bf16[32,12,896]{2,1,0:T(8,128)(2,1)}), bf16[32,12,896]{2,1,0:T(8,128)(2,1)}, u32[]{:S(2)}, u32[]{:S(2)}) %all-to-all-start) | async-done | bytes 688160 | tf_op jit(solution)/shard_map/all_to_all | solution.py:155
  62.7 13.6 %all-gather = bf16[24,12,896]{2,1,0:T(8,128)(2,1)S(1)} all-gather(bf16[6,12,896]{2,1,0:T(8,128)(2,1)S(1)} %get-tuple-element.9), channel_id=2, replica_groups=mesh['seq'=32,'mp_0'=4,'mp_1'=2] {'mp_0'}, dimensions={0}, use_global_device_ids=true | all-gather | bytes 645120 | tf_op jit(solution)/shard_map/all_gather | solution.py:24
  76.2 2.8 %all_gather.13 = bf16[8,6,12,896]{3,2,1,0:T(8,128)(2,1)S(1)} all-gather(bf16[4,6,12,896]{3,2,1,0:T(8,128)(2,1)S(1)} %bitcast.93), channel_id=1, replica_groups=mesh['seq'=32,'mp_0'=4,'mp_1'=2] {'mp_1'}, dimensions={0}, use_global_device_ids=true | all-gather | bytes 1548288 | tf_op jit(solution)/shard_map/all_gather | solution.py:24
  79.2 17.9 %all_gather.15 = bf16[8,6,12,896]{3,2,0,1:T(8,128)(2,1)S(1)} all-gather(bf16[2,6,12,896]{3,2,0,1:T(8,128)(2,1)S(1)} %copy.99), channel_id=1, replica_groups=mesh['seq'=32,'mp_0'=4,'mp_1'=2] {'mp_0'}, dimensions={0}, use_global_device_ids=true | all-gather | bytes 1290240 | tf_op jit(solution)/shard_map/all_gather | solution.py:24
  99.1 4.6 %reshape.204 = bf16[12,96,896]{2,1,0:T(8,128)(2,1)} reshape(bf16[12,8,12,896]{3,2,1,0:T(8,128)(2,1)} %maximum_bitcast_fusion) | data formatting | bytes 4128768 | tf_op jit(solution)/shard_map/reshape | solution.py:34
  103.7 3.2 %convolution_convert_fusion = bf16[12,96,512]{2,1,0:T(8,128)(2,1)S(1)} fusion(bf16[12,96,896]{2,1,0:T(8,128)(2,1)} %reshape.204, bf16[896,256]{1,0:T(8,128)(2,1)} %param.23, bf16[896,256]{1,0:T(8,128)(2,1)} %param.22), kind=kOutput, calls=%fused_computation.36 | convolution fusion | flops 1059389440 | bytes 4161536 | tf_op jit(solution)/shard_map/nle,ef->nlf/dot_general | solution.py:158
  108.0 2.5 %reshape.207 = bf16[6,192,2,128]{3,2,1,0:T(2,128)(2,1)} reshape(bf16[12,96,256]{2,1,0:T(8,128)(2,1)} %get-tuple-element.6) | data formatting | bytes 1179648 | tf_op jit(solution)/shard_map/reshape | solution.py:171
  110.6 2.6 %fusion.87 = f32[6,2,64,192]{3,2,1,0:T(8,128)} fusion(bf16[6,192,2,128]{3,2,1,0:T(2,128)(2,1)} %reshape.207, bf16[6,64,2,128]{3,2,1,0:T(2,128)(2,1)} %reshape.206), kind=kOutput, calls=%fused_computation.92 | convolution fusion | flops 38044608 | bytes 1376256 | tf_op jit(solution)/shard_map/div | solution.py:179
  113.2 2.6 %fusion.32 = f32[6,2,64,192]{3,2,1,0:T(8,128)} fusion(bf16[6,192,2,128]{3,2,1,0:T(2,128)(2,1)} %reshape.207, bf16[6,64,2,128]{3,2,1,0:T(2,128)(2,1)} %reshape.206), kind=kOutput, calls=%fused_computation.44 | convolution fusion | flops 37896192 | bytes 1376256 | tf_op jit(solution)/shard_map/cqhd,ckhd->chqk/dot_general | solution.py:175
  115.8 2.5 reshape.205
  118.3 2.6 %fusion.53 = bf16[6,64,2,128]{3,1,2,0:T(8,128)(2,1)} fusion(bf16[6,192,2,128]{3,2,1,0:T(2,128)(2,1)} %reshape.205, f32[6,2,64,192]{3,2,1,0:T(8,128)} %fusion.32), kind=kOutput, calls=%fused_computation.57 | convolution fusion | flops 38142912 | bytes 1376256 | tf_op jit(solution)/shard_map/chqk,ckhd->cqhd/dot_general | solution.py:182
  120.9 2.6 %fusion.78 = f32[6,2,64,192]{3,2,1,0:T(8,128)} fusion(bf16[6,192,2,128]{3,2,1,0:T(2,128)(2,1)} %reshape.205, bf16[6,64,2,128]{3,2,1,0:T(2,128)(2,1)} %reshape.209), kind=kOutput, calls=%fused_computation.83 | convolution fusion | flops 37748736 | bytes 1376256 | tf_op jit(solution)/shard_map/cqhd,ckhd->chqk/dot_general | solution.py:194
  123.4 3.2 %fusion.54 = bf16[6,64,2,128]{3,1,2,0:T(8,128)(2,1)} fusion(f32[6,2,64,192]{3,2,1,0:T(8,128)} %fusion.87, f32[6,2,64,192]{3,2,1,0:T(8,128)} %fusion.78, bf16[6,192,2,128]{3,2,1,0:T(2,128)(2,1)} %reshape.207), kind=kOutput, calls=%fused_computation.58 | convolution fusion | flops 38585280 | bytes 1966080 | tf_op jit(solution)/shard_map/chqk,ckhd->cqhd/dot_general | solution.py:204
  134.4 3.3 %fusion.42 = bf16[6,192,2,128]{3,1,2,0:T(8,128)(2,1)} fusion(f32[6,2,64,192]{3,2,1,0:T(8,128)} %fusion.87, f32[6,2,64,192]{3,2,1,0:T(8,128)} %fusion.78, bf16[6,64,2,128]{3,2,1,0:T(2,128)(2,1)} %reshape.206), kind=kOutput, calls=%fused_computation.50 | convolution fusion | flops 38781888 | bytes 1966080 | tf_op jit(solution)/shard_map/chqk,cqhd->ckhd/dot_general | solution.py:208
  137.8 2.5 copy.109
  140.3 2.8 %reshape.211 = bf16[12,96,256]{2,1,0:T(8,128)(2,1)} reshape(bf16[6,192,2,128]{3,2,1,0:T(2,128)(2,1)} %copy.109) | data formatting | bytes 1179648 | tf_op jit(solution)/shard_map/reshape | solution.py:211
  143.1 2.8 %fusion.43 = bf16[6,192,2,128]{3,1,2,0:T(8,128)(2,1)} fusion(bf16[6,64,2,128]{3,2,1,0:T(2,128)(2,1)} %reshape.209, f32[6,2,64,192]{3,2,1,0:T(8,128)} %fusion.32), kind=kOutput, calls=%fused_computation.51 | convolution fusion | flops 38339520 | bytes 1376256 | tf_op jit(solution)/shard_map/chqk,cqhd->ckhd/dot_general | solution.py:200
  145.9 2.5 copy.111
  148.4 2.8 %reshape.212 = bf16[12,96,256]{2,1,0:T(8,128)(2,1)} reshape(bf16[6,192,2,128]{3,2,1,0:T(2,128)(2,1)} %copy.111) | data formatting | bytes 1179648 | tf_op jit(solution)/shard_map/reshape | solution.py:212
  155.4 4.5 %reshape.213 = bf16[12,8,12,896]{3,2,1,0:T(8,128)(2,1)} reshape(bf16[12,96,896]{2,1,0:T(8,128)(2,1)} %add_convert_fusion) | data formatting | bytes 4128768 | tf_op jit(solution)/shard_map/reshape | solution.py:49
  162.0 36.9 %all_to_all.15 = bf16[8,12,12,896]{3,2,1,0:T(8,128)(2,1)S(1)} all-to-all(bf16[8,12,12,896]{3,2,1,0:T(8,128)(2,1)S(1)} %copy.112), channel_id=1, replica_groups=mesh['seq'=32,'mp_0'=4,'mp_1'=2] {'mp_0','mp_1'}, dimensions={0} | all-to-all | bytes 4128768 | tf_op jit(solution)/shard_map/all_to_all | solution.py:55
  200.2 6.1 %fusion.68 = (f32[12,12]{1,0:T(8,128)}, f32[12,12,896]{2,1,0:T(8,128)}) fusion(f32[12,12]{1,0:T(8,128)} %copy-done.6, bf16[12,12,896]{2,1,0:T(8,128)(2,1)S(1)} %gather_fusion.1, pred[12]{0:T(512)(128)(4,1)} %compare_and_fusion.1, f32[896]{0:T(1024)} %param.18, bf16[896,1792]{1,0:T(8,128)(2,1)S(1)} %copy-done, bf16[1792,896]{1,0:T(8,128)(2,1)} %param.20, ...), kind=kOutput, calls=%fused_computation.73 | convolution fusion | flops 928069504 | bytes 8749708 | tf_op jit(solution)/shard_map/nlf,ef->nle/dot_general | solution.py:100
  209.6 31.8 %all_to_all.16 = bf16[32,12,896]{2,1,0:T(8,128)(2,1)S(1)} all-to-all(bf16[32,12,896]{2,1,0:T(8,128)(2,1)S(1)} %copy.114), channel_id=1, replica_groups=mesh['seq'=32,'mp_0'=4,'mp_1'=2] {'seq'}, dimensions={0} | all-to-all | bytes 1376256 | tf_op jit(solution)/shard_map/all_to_all | solution.py:226
  (102 shorter events, 52.2 us)
Async XLA Ops:
  7.2 50.3 %copy-start = (bf16[896,1792]{1,0:T(8,128)(2,1)S(1)}, bf16[896,1792]{1,0:T(8,128)(2,1)}, u32[]{:S(2)}) copy-start(bf16[896,1792]{1,0:T(8,128)(2,1)} %param.19) | copy-start | bytes 9633796
  11.1 0.6 copy-start.15
  16.6 13.6 %copy-start.9 = (f32[2048]{0:T(1024)S(1)}, f32[2048]{0:T(1024)}, u32[]{:S(2)}) copy-start(f32[2048]{0:T(1024)} %param.17) | copy-start | bytes 24580
  16.6 37.4 %all-to-all-start = ((bf16[32,12,896]{2,1,0:T(8,128)(2,1)}), bf16[32,12,896]{2,1,0:T(8,128)(2,1)}, u32[]{:S(2)}, u32[]{:S(2)}) async-start(bf16[32,12,896]{2,1,0:T(8,128)(2,1)} %broadcast_select_fusion), calls=%async_computation | async-start | bytes 1835008 | tf_op jit(solution)/shard_map/all_to_all | solution.py:155
  28.2 214.2 %reduce-scatter.2.cloned.1.call-start = ((), (), s32[]{:S(2)}) async-start(), calls=%async_computation.4 | async-start | bytes 3538944 | tf_op jit(solution)/shard_map/reduce_scatter | solution.py:61
  28.4 4.9 %copy-start.18 = (pred[384]{0:T(512)(128)(4,1)}, pred[384]{0:T(512)(128)(4,1)S(1)}, u32[]{:S(2)}) copy-start(pred[384]{0:T(512)(128)(4,1)S(1)} %broadcast_in_dim.71) | copy-start | bytes 1156
  30.2 2.3 copy-start.7
  36.5 0.6 copy-start.12
  56.9 0.6 copy-start.6
  57.5 1.8 copy-start.11
  57.5 1.9 copy-start.17
  59.4 1.2 copy-start.3
  126.6 4.3 %copy-start.1 = (bf16[384,2048]{1,0:T(8,128)(2,1)S(1)}, bf16[384,2048]{1,0:T(8,128)(2,1)}, u32[]{:S(2)}) copy-start(bf16[384,2048]{1,0:T(8,128)(2,1)} %param.13) | copy-start | bytes 4718596
  126.6 4.3 %copy-start.4 = (bf16[2048,256]{1,0:T(8,128)(2,1)S(1)}, bf16[2048,256]{1,0:T(8,128)(2,1)}, u32[]{:S(2)}) copy-start(bf16[2048,256]{1,0:T(8,128)(2,1)} %param.21) | copy-start | bytes 3145732
  126.6 4.3 %copy-start.8 = (f32[384]{0:T(512)S(1)}, f32[384]{0:T(512)}, u32[]{:S(2)}) copy-start(f32[384]{0:T(512)} %copy-done.7) | copy-start | bytes 4612
  126.6 4.3 %copy-start.10 = (f32[2048]{0:T(1024)S(1)}, f32[2048]{0:T(1024)}, u32[]{:S(2)}) copy-start(f32[2048]{0:T(1024)} %param.17) | copy-start | bytes 24580
  151.1 2.1 copy-start.2
  151.1 2.1 copy-start.5
  206.3 2.2 copy-start.13
  209.4 32.0 %copy-start.14 = (pred[32]{0:T(512)(128)(4,1)S(1)}, pred[32]{0:T(512)(128)(4,1)}, u32[]{:S(2)}) copy-start(pred[32]{0:T(512)(128)(4,1)} %get-tuple-element.3) | copy-start | bytes 100
  209.4 32.0 %copy-start.16 = (s32[32]{0:T(128)S(1)}, s32[32]{0:T(128)}, u32[]{:S(2)}) copy-start(s32[32]{0:T(128)} %copy-done.15) | copy-start | bytes 388
Sparse Core Ops, SparseCore 0:
  134.6 33.3 reduce-scatter.1
where the time goes:
time: 252 us; the launch traced here: 251 us
  blocking collectives  105 us (42%)
  matrix products  44.9 us (18%)
  local copies, waits for them, and re-layouts  41 us (16%)
  other arithmetic  17.9 us (7%)
  waiting for transfers between devices  16.4 us (7%)
  between operations  14.4 us (6%)
  starting transfers between devices  11.6 us (5%)
    all_to_all x1, blocking collectives, summed_on_arrival(): tiles = lax.all_to_all(split_up(x, dim, devices), axis, 0, 0, tiled=True)  36.9 us
    all_gather x4, blocking collectives, gather_in_order(): tiles = lax.all_gather(tiles, axes[k], axis=0, tiled=True)  36.3 us
    all_to_all x1, blocking collectives, body(): lax.all_to_all(returned.astype(jnp.bfloat16), 'seq', split_axis=0, concat...  31.8 us
    all_to_all x1, waiting for transfers between devices, body(): lax.all_to_all(outgoing, 'seq', split_axis=0, concat_axis=0, tiled=True)  16.4 us
    all_to_all x1, starting transfers between devices, body(): lax.all_to_all(outgoing, 'seq', split_axis=0, concat_axis=0, tiled=True)  11.5 us
    dot_general x1, matrix products, encode_back(): jnp.einsum('nlf,ef->nle', grad_pre, w_in, preferred_element_type=jnp.floa...  6.08 us
  transfers between devices with their start and end apart: 2, of which 1 were waited for; matrix products, arithmetic and copies ran while one was open for 19% of the time, Pallas kernels for 0%

commit v1 on v0

--- a/solution.py
+++ b/solution.py
@@ -21,7 +21,20 @@
 def gather_in_order(x, axes, sequence):
     tiles = x[None]
     for k in sequence:
-        tiles = lax.all_gather(tiles, axes[k], axis=0, tiled=True)
+
+        def _replace_cycles(u, ax_name):
+            kept_arr = jnp.concatenate(
+                lax.all_to_all(
+                    jnp.stack([u for _ in range(lax.axis_size(ax_name))], axis=0),
+                    axis_name=ax_name,
+                    split_axis=0,
+                    concat_axis=0,
+                ),
+                axis=0,
+            )
+            return kept_arr
+
+        tiles = _replace_cycles(tiles, axes[k])
     block = [lax.axis_size(axes[k]) for k in reversed(sequence)]
     tiles = tiles.reshape(*block, *x.shape)
     turned = sorted(range(len(sequence)), key=lambda place: sequence[len(sequence) - 1 - place])

time: 252 us -> 278 us (1.10)
  blocking collectives: 105 us -> 80.5 us
  local copies, waits for them, and re-layouts: 41 us -> 64.7 us
  waiting for transfers between devices: 16.4 us -> 30.1 us
  starting transfers between devices: 11.6 us -> 20.2 us
    all_gather x4 -> x0, blocking collectives: 36.3 us -> none  [gather_in_order(): tiles = lax.all_gather(tiles, axes[k], axis=0, tiled=True)]
    all_to_all x0 -> x2, blocking collectives: none -> 10.1 us  [_replace_cycles(): lax.all_to_all(jnp.stack([u for _ in range(lax.axis_size(ax_name))], axis...]
    all_to_all x0 -> x2, starting transfers between devices: none -> 8.53 us  [_replace_cycles(): lax.all_to_all(jnp.stack([u for _ in range(lax.axis_size(ax_name))], axis...]
    another operation x0 -> x5, local copies, waits for them, and re-layouts: none -> 8.29 us  [the longest x4 4.86 us: _replace_cycles(): jnp.stack([u for _ in range(lax.axis_size(ax_name))], axis=0)]
    all_to_all x1, waiting for transfers between devices: 16.4 us -> 24.5 us  [body(): lax.all_to_all(outgoing, 'seq', split_axis=0, concat_axis=0, tiled=True)]
    all_to_all x0 -> x2, waiting for transfers between devices: none -> 5.51 us  [_replace_cycles(): lax.all_to_all(jnp.stack([u for _ in range(lax.axis_size(ax_name))], axis...]
    reshape x0 -> x1, local copies, waits for them, and re-layouts: none -> 3.42 us  [gather_in_order(): tiles.transpose(*turned, *range(len(sequence), tiles.ndim))]
    all_to_all x0 -> x1, local copies, waits for them, and re-layouts: none -> 2.95 us  [_replace_cycles(): lax.all_to_all(jnp.stack([u for _ in range(lax.axis_size(ax_name))], axis...]
  transfers between devices with their start and end apart: 2 -> 4, of which waited for: 1 -> 2; matrix products, arithmetic and copies ran while one was open for 19% -> 23% of each run, Pallas kernels for 0% -> 0%
where the time goes in v1:
time: 278 us; the launch traced here: 277 us
  blocking collectives  80.5 us (29%)
  local copies, waits for them, and re-layouts  64.7 us (23%)
  matrix products  46.2 us (17%)
  waiting for transfers between devices  30.1 us (11%)
  other arithmetic  20.5 us (7%)
  starting transfers between devices  20.2 us (7%)
  between operations  14.4 us (5%)
    all_to_all x1, blocking collectives, summed_on_arrival(): tiles = lax.all_to_all(split_up(x, dim, devices), axis, 0, 0, tiled=True)  38.6 us
    all_to_all x1, blocking collectives, body(): lax.all_to_all(returned.astype(jnp.bfloat16), 'seq', split_axis=0, concat...  31.8 us
    all_to_all x1, waiting for transfers between devices, body(): lax.all_to_all(outgoing, 'seq', split_axis=0, concat_axis=0, tiled=True)  24.5 us
    all_to_all x1, starting transfers between devices, body(): lax.all_to_all(outgoing, 'seq', split_axis=0, concat_axis=0, tiled=True)  11.4 us
    all_to_all x2, blocking collectives, _replace_cycles(): lax.all_to_all(jnp.stack([u for _ in range(lax.axis_size(ax_name))], axis...  10.1 us
    all_to_all x2, starting transfers between devices, _replace_cycles(): lax.all_to_all(jnp.stack([u for _ in range(lax.axis_size(ax_name))], axis...  8.53 us
    dot_general x1, matrix products, encode_back(): jnp.einsum('nlf,ef->nle', grad_pre, w_in, preferred_element_type=jnp.floa...  6.08 us
  transfers between devices with their start and end apart: 4, of which 2 were waited for; matrix products, arithmetic and copies ran while one was open for 23% of the time, Pallas kernels for 0%

profile of v1, /device:TPU:32, one launch (start us, length us, event | category | flops | bytes accessed | tf_op | source)
XLA Modules:
  0.0 276.5 jit_solution(403814047104822341)
XLA Ops:
  16.6 11.4 %all-to-all-start = ((bf16[32,12,896]{2,1,0:T(8,128)(2,1)}), bf16[32,12,896]{2,1,0:T(8,128)(2,1)}, u32[]{:S(2)}, u32[]{:S(2)}) async-start(bf16[32,12,896]{2,1,0:T(8,128)(2,1)} %broadcast_select_fusion), calls=%async_computation | async-start | bytes 1835008 | tf_op jit(solution)/shard_map/all_to_all | solution.py:168
  29.4 24.5 %all-to-all-done = bf16[32,12,896]{2,1,0:T(8,128)(2,1)} async-done(((bf16[32,12,896]{2,1,0:T(8,128)(2,1)}), bf16[32,12,896]{2,1,0:T(8,128)(2,1)}, u32[]{:S(2)}, u32[]{:S(2)}) %all-to-all-start) | async-done | bytes 688160 | tf_op jit(solution)/shard_map/all_to_all | solution.py:168
  60.5 4.7 %all_to_all.35 = bf16[2,1,6,12,896]{4,3,2,1,0:T(8,128)(2,1)} all-to-all(bf16[2,1,6,12,896]{4,3,2,1,0:T(8,128)(2,1)S(1)} %pad_maximum_fusion.2), channel_id=1, replica_groups=mesh['seq'=32,'mp_0'=4,'mp_1'=2] {'mp_1'}, dimensions={0} | all-to-all | bytes 516096 | tf_op jit(solution)/shard_map/all_to_all | solution.py:27
  66.2 4.3 %all-to-all-start.1 = ((bf16[4,1,6,12,896]{4,3,2,1,0:T(8,128)(2,1)}), bf16[4,1,6,12,896]{4,3,2,1,0:T(8,128)(2,1)}, u32[]{:S(2)}, u32[]{:S(2)}) async-start(bf16[4,1,6,12,896]{4,3,2,1,0:T(8,128)(2,1)} %stack.12), calls=%async_computation.1 | async-start | bytes 1376256 | tf_op jit(solution)/shard_map/all_to_all | solution.py:27
  76.7 5.5 %all-to-all-done.1 = bf16[4,1,6,12,896]{4,3,2,1,0:T(8,128)(2,1)} async-done(((bf16[4,1,6,12,896]{4,3,2,1,0:T(8,128)(2,1)}), bf16[4,1,6,12,896]{4,3,2,1,0:T(8,128)(2,1)}, u32[]{:S(2)}, u32[]{:S(2)}) %all-to-all-start.1) | async-done | bytes 516128 | tf_op jit(solution)/shard_map/all_to_all | solution.py:27
  84.4 5.4 %all_to_all.36 = bf16[2,4,6,12,896]{4,1,3,2,0:T(4,128)(2,1)} all-to-all(bf16[2,4,6,12,896]{4,1,3,2,0:T(4,128)(2,1)S(1)} %copy.123), channel_id=1, replica_groups=mesh['seq'=32,'mp_0'=4,'mp_1'=2] {'mp_1'}, dimensions={0} | all-to-all | bytes 2064384 | tf_op jit(solution)/shard_map/all_to_all | solution.py:27
  91.3 4.2 %all-to-all-start.4 = ((bf16[4,2,6,12,896]{4,1,3,2,0:T(2,128)(2,1)}), bf16[4,2,6,12,896]{4,1,3,2,0:T(2,128)(2,1)}, u32[]{:S(2)}, u32[]{:S(2)}) async-start(bf16[4,2,6,12,896]{4,1,3,2,0:T(2,128)(2,1)} %stack.15), calls=%async_computation.4 | async-start | bytes 2064384 | tf_op jit(solution)/shard_map/all_to_all | solution.py:27
  97.0 3.0 %fusion.47 = bf16[384,256]{1,0:T(8,128)(2,1)} fusion(bf16[2048,256]{1,0:T(8,128)(2,1)} %param.21, bf16[384,2048]{1,0:T(8,128)(2,1)} %param.13, f32[2048]{0:T(1024)} %param.17, f32[384]{0:T(512)S(1)} %add_rsqrt_fusion.1), kind=kOutput, calls=%fused_computation.54 | convolution fusion | flops 405897216 | bytes 2827776 | tf_op jit(solution)/shard_map/dot_general | solution.py:180
  101.7 3.0 %fusion.50 = bf16[384,256]{1,0:T(8,128)(2,1)} fusion(bf16[256,2048]{1,0:T(8,128)(2,1)} %param.24, bf16[384,2048]{1,0:T(8,128)(2,1)} %param.25, pred[384]{0:T(512)(128)(4,1)} %broadcast_in_dim.45), kind=kOutput, calls=%fused_computation.55 | convolution fusion | flops 403537920 | bytes 2818432 | tf_op jit(solution)/shard_map/dot_general | solution.py:91
  106.3 3.0 %copy.124 = bf16[4,2,6,12,896]{4,1,0,3,2:T(2,128)(2,1)} copy(bf16[4,2,6,12,896]{4,0,3,2,1:T(4,128)(2,1)} %bitcast.94) | data formatting | bytes 2064384 | tf_op jit(solution)/shard_map/transpose | solution.py:41
  109.4 3.4 %reshape.203 = bf16[8,6,12,896]{3,0,2,1:T(8,128)(2,1)} reshape(bf16[4,2,6,12,896]{4,1,0,3,2:T(2,128)(2,1)} %copy.124) | data formatting | bytes 2064384 | tf_op jit(solution)/shard_map/reshape | solution.py:41
  112.8 2.9 %copy.126 = bf16[4,2,6,12,896]{4,1,0,3,2:T(2,128)(2,1)} copy(bf16[4,2,6,12,896]{4,1,3,2,0:T(2,128)(2,1)} %all-to-all-done.4) | data formatting | bytes 2064384 | tf_op jit(solution)/shard_map/all_to_all | solution.py:27
  115.7 3.4 %reshape_reshape_reshape.3 = bf16[8,6,12,896]{3,0,2,1:T(8,128)(2,1)} reshape(bf16[4,2,6,12,896]{4,1,0,3,2:T(2,128)(2,1)} %copy.126) | data formatting | bytes 2064384 | tf_op jit(solution)/shard_map/reshape;reshape;reshape | solution.py:41
  122.9 4.6 %reshape.204 = bf16[12,96,896]{2,1,0:T(8,128)(2,1)} reshape(bf16[12,8,12,896]{3,2,1,0:T(8,128)(2,1)} %copy.127) | data formatting | bytes 4128768 | tf_op jit(solution)/shard_map/reshape | solution.py:47
  127.6 3.2 %convolution_convert_fusion = bf16[12,96,512]{2,1,0:T(8,128)(2,1)S(1)} fusion(bf16[12,96,896]{2,1,0:T(8,128)(2,1)} %reshape.204, bf16[896,256]{1,0:T(8,128)(2,1)} %param.23, bf16[896,256]{1,0:T(8,128)(2,1)} %param.22), kind=kOutput, calls=%fused_computation.36 | convolution fusion | flops 1059389440 | bytes 4161536 | tf_op jit(solution)/shard_map/nle,ef->nlf/dot_general | solution.py:171
  147.3 3.2 %fusion.54 = bf16[6,64,2,128]{3,1,2,0:T(8,128)(2,1)} fusion(f32[6,2,64,192]{3,2,1,0:T(8,128)} %fusion.87, f32[6,2,64,192]{3,2,1,0:T(8,128)} %fusion.78, bf16[6,192,2,128]{3,2,1,0:T(2,128)(2,1)} %reshape.207), kind=kOutput, calls=%fused_computation.59 | convolution fusion | flops 38585280 | bytes 1966080 | tf_op jit(solution)/shard_map/chqk,ckhd->cqhd/dot_general | solution.py:217
  158.3 3.3 %fusion.42 = bf16[6,192,2,128]{3,1,2,0:T(8,128)(2,1)} fusion(f32[6,2,64,192]{3,2,1,0:T(8,128)} %fusion.87, f32[6,2,64,192]{3,2,1,0:T(8,128)} %fusion.78, bf16[6,64,2,128]{3,2,1,0:T(2,128)(2,1)} %reshape.206), kind=kOutput, calls=%fused_computation.51 | convolution fusion | flops 38781888 | bytes 1966080 | tf_op jit(solution)/shard_map/chqk,cqhd->ckhd/dot_general | solution.py:221
  164.1 2.8 reshape.211
  166.8 2.8 %fusion.43 = bf16[6,192,2,128]{3,1,2,0:T(8,128)(2,1)} fusion(bf16[6,64,2,128]{3,2,1,0:T(2,128)(2,1)} %reshape.209, f32[6,2,64,192]{3,2,1,0:T(8,128)} %fusion.32), kind=kOutput, calls=%fused_computation.52 | convolution fusion | flops 38339520 | bytes 1376256 | tf_op jit(solution)/shard_map/chqk,cqhd->ckhd/dot_general | solution.py:213
  172.1 2.8 %reshape.212 = bf16[12,96,256]{2,1,0:T(8,128)(2,1)} reshape(bf16[6,192,2,128]{3,2,1,0:T(2,128)(2,1)} %copy.139) | data formatting | bytes 1179648 | tf_op jit(solution)/shard_map/reshape | solution.py:225
  179.1 4.6 %reshape.213 = bf16[12,8,12,896]{3,2,1,0:T(8,128)(2,1)} reshape(bf16[12,96,896]{2,1,0:T(8,128)(2,1)} %add_convert_fusion) | data formatting | bytes 4128768 | tf_op jit(solution)/shard_map/reshape | solution.py:62
  185.7 38.6 %all_to_all.37 = bf16[8,12,12,896]{3,2,1,0:T(8,128)(2,1)S(1)} all-to-all(bf16[8,12,12,896]{3,2,1,0:T(8,128)(2,1)S(1)} %copy.140), channel_id=1, replica_groups=mesh['seq'=32,'mp_0'=4,'mp_1'=2] {'mp_0','mp_1'}, dimensions={0} | all-to-all | bytes 4128768 | tf_op jit(solution)/shard_map/all_to_all | solution.py:68
  225.7 6.1 %fusion.68 = (f32[12,12]{1,0:T(8,128)}, f32[12,12,896]{2,1,0:T(8,128)}) fusion(f32[12,12]{1,0:T(8,128)} %copy-done.7, bf16[12,12,896]{2,1,0:T(8,128)(2,1)S(1)} %gather_fusion.1, pred[12]{0:T(512)(128)(4,1)} %compare_and_fusion.1, f32[896]{0:T(1024)} %param.18, bf16[896,1792]{1,0:T(8,128)(2,1)S(1)} %copy-done, bf16[1792,896]{1,0:T(8,128)(2,1)} %param.20, ...), kind=kOutput, calls=%fused_computation.74 | convolution fusion | flops 928069504 | bytes 8749708 | tf_op jit(solution)/shard_map/nlf,ef->nle/dot_general | solution.py:113
  235.1 31.8 %all_to_all.38 = bf16[32,12,896]{2,1,0:T(8,128)(2,1)S(1)} all-to-all(bf16[32,12,896]{2,1,0:T(8,128)(2,1)S(1)} %copy.142), channel_id=1, replica_groups=mesh['seq'=32,'mp_0'=4,'mp_1'=2] {'seq'}, dimensions={0} | all-to-all | bytes 1376256 | tf_op jit(solution)/shard_map/all_to_all | solution.py:239
  (111 shorter events, 79.6 us)
Async XLA Ops:
  7.2 50.2 %copy-start = (bf16[896,1792]{1,0:T(8,128)(2,1)S(1)}, bf16[896,1792]{1,0:T(8,128)(2,1)}, u32[]{:S(2)}) copy-start(bf16[896,1792]{1,0:T(8,128)(2,1)} %param.19) | copy-start | bytes 9633796
  11.1 0.6 copy-start.15
  16.6 37.3 %all-to-all-start = ((bf16[32,12,896]{2,1,0:T(8,128)(2,1)}), bf16[32,12,896]{2,1,0:T(8,128)(2,1)}, u32[]{:S(2)}, u32[]{:S(2)}) async-start(bf16[32,12,896]{2,1,0:T(8,128)(2,1)} %broadcast_select_fusion), calls=%async_computation | async-start | bytes 1835008 | tf_op jit(solution)/shard_map/all_to_all | solution.py:168
  28.2 0.6 copy-start.12
  56.7 0.6 copy-start.7
  57.3 1.8 copy-start.11
  57.3 1.9 copy-start.17
  59.3 1.2 copy-start.3
  66.2 16.1 %all-to-all-start.1 = ((bf16[4,1,6,12,896]{4,3,2,1,0:T(8,128)(2,1)}), bf16[4,1,6,12,896]{4,3,2,1,0:T(8,128)(2,1)}, u32[]{:S(2)}, u32[]{:S(2)}) async-start(bf16[4,1,6,12,896]{4,3,2,1,0:T(8,128)(2,1)} %stack.12), calls=%async_computation.1 | async-start | bytes 1376256 | tf_op jit(solution)/shard_map/all_to_all | solution.py:27
  83.8 5.9 %copy-start.5 = (bf16[2,6,12,896]{3,0,2,1:T(2,128)(2,1)S(1)}, bf16[2,6,12,896]{3,0,2,1:T(2,128)(2,1)}, u32[]{:S(2)}) copy-start(bf16[2,6,12,896]{3,0,2,1:T(2,128)(2,1)} %copy.125) | copy-start | bytes 774148
  91.3 21.5 %all-to-all-start.4 = ((bf16[4,2,6,12,896]{4,1,3,2,0:T(2,128)(2,1)}), bf16[4,2,6,12,896]{4,1,3,2,0:T(2,128)(2,1)}, u32[]{:S(2)}, u32[]{:S(2)}) async-start(bf16[4,2,6,12,896]{4,1,3,2,0:T(2,128)(2,1)} %stack.15), calls=%async_computation.4 | async-start | bytes 2064384 | tf_op jit(solution)/shard_map/all_to_all | solution.py:27
  95.5 172.3 %reduce-scatter.2.cloned.1.call-start = ((), (), s32[]{:S(2)}) async-start(), calls=%async_computation.8 | async-start | bytes 3538944 | tf_op jit(solution)/shard_map/reduce_scatter | solution.py:74
  96.4 0.6 copy-start.8
  150.5 4.3 %copy-start.1 = (bf16[384,2048]{1,0:T(8,128)(2,1)S(1)}, bf16[384,2048]{1,0:T(8,128)(2,1)}, u32[]{:S(2)}) copy-start(bf16[384,2048]{1,0:T(8,128)(2,1)} %param.13) | copy-start | bytes 4718596
  150.5 4.3 %copy-start.4 = (bf16[2048,256]{1,0:T(8,128)(2,1)S(1)}, bf16[2048,256]{1,0:T(8,128)(2,1)}, u32[]{:S(2)}) copy-start(bf16[2048,256]{1,0:T(8,128)(2,1)} %param.21) | copy-start | bytes 3145732
  150.5 4.3 %copy-start.9 = (f32[384]{0:T(512)S(1)}, f32[384]{0:T(512)}, u32[]{:S(2)}) copy-start(f32[384]{0:T(512)} %copy-done.8) | copy-start | bytes 4612
  150.5 4.3 %copy-start.10 = (f32[2048]{0:T(1024)S(1)}, f32[2048]{0:T(1024)}, u32[]{:S(2)}) copy-start(f32[2048]{0:T(1024)} %param.17) | copy-start | bytes 24580
  174.9 2.1 copy-start.2
  174.9 2.1 copy-start.6
  231.8 2.2 copy-start.13
  234.8 32.0 %copy-start.14 = (pred[32]{0:T(512)(128)(4,1)S(1)}, pred[32]{0:T(512)(128)(4,1)}, u32[]{:S(2)}) copy-start(pred[32]{0:T(512)(128)(4,1)} %get-tuple-element.3) | copy-start | bytes 100
  234.9 32.0 %copy-start.16 = (s32[32]{0:T(128)S(1)}, s32[32]{0:T(128)}, u32[]{:S(2)}) copy-start(s32[32]{0:T(128)} %copy-done.15) | copy-start | bytes 388
Sparse Core Ops, SparseCore 0:
  158.4 34.9 reduce-scatter.1
